TPU v7x, 128 devices: a whole 4x4x4 slice. The times are simulated.
128 devices in a mesh: dp: 4 (over z_hi, core), ep: 32 (over x, z_lo, y).
Axes of the slice: x: 4, y: 4, z: 4 (z_hi: 2, z_lo: 2; z = z_hi * 2 + z_lo), core: 2. Of those that a mesh axis runs over, the one named last changes fastest.
Arguments:
- tokens: bfloat16 [16384, 2048], P(('dp', 'ep')), parts along dimension 0, may hold values from -6 to 6
- expert_ids: int32 [16384, 8], P(('dp', 'ep')), parts along dimension 0, may hold values from 0 to 63, all different within a row; in each aligned block of 32 rows (0 to 31, 32 to 63, ...) at most 8 rows name the same one
- gate_nums: int32 [16384, 8], P(('dp', 'ep')), parts along dimension 0, may hold values from 64 to 1023
- w_gate: bfloat16 [64, 2048, 768], P('ep'), may hold values from -0.125 to 0.125
- w_up: bfloat16 [64, 2048, 768], P('ep'), may hold values from -0.125 to 0.125
- w_down: bfloat16 [64, 768, 2048], P('ep'), may hold values from -0.21875 to 0.21875
Outputs:
- mixed: bfloat16 [16384, 2048], P(('dp', 'ep')), parts along dimension 0
There are 4 independent parts, one for each index of `dp`. A program takes and returns all parts, laid end to end along the dimension named above; an argument that names none is the same for every part. Nothing has to cross between parts.
Inputs may be any that keep to these rules, and one draw needn't show every extreme that they name: `expert_ids`: each row names 8 different experts. In every aligned block of 32 rows no expert is named by more than 8 rows, a bound that some block reaches.
All inputs are finite; a program needn't handle non-finite values.
Results may differ from a plain program's by a relative error of at most 0.008.
Values may be sent and summed in bfloat16 or wider, within the bound.
A program may use at most 128 MiB of HBM per device.

v0:
```python
import jax
import jax.numpy as jnp
from jax import lax
from jax.experimental import pallas as pl
from jax.experimental.pallas import tpu as pltpu
from jax.sharding import PartitionSpec as P

MESH = pl.DeviceIdType.MESH
BF = jnp.bfloat16
F32 = jnp.float32
D = 2048
FF = 768
TOK = 128
HALF = 64
CAP = 32
ORDER = (0, 3, 1, 2)
BACK = (2, 1, 3, 0)


def neighbours():
    dp, ep = lax.axis_index("dp"), lax.axis_index("ep")
    z_hi, core = dp // 2, dp % 2
    x, z_lo, y = ep // 8, (ep // 4) % 2, ep % 4
    z = z_hi * 2 + z_lo
    a = (1 - core) * x + core * y
    b = (1 - core) * y + core * x

    def device(a, b, z):
        px = (1 - core) * a + core * b
        py = (1 - core) * b + core * a
        return ((z // 2) * 2 + core, (px * 2 + z % 2) * 4 + py)

    up = z + 1 - 2 * (z % 2)
    down = (z + 3 + 2 * (z % 2)) % 4
    zp = (1 - core) * up + core * down
    where = {
        "a+": device((a + 1) % 4, b, z),
        "a-": device((a + 3) % 4, b, z),
        "b+": device(a, (b + 1) % 4, z),
        "b-": device(a, (b + 3) % 4, z),
        "z": device(a, b, zp),
    }
    return where, ep, where["z"][1]


def kernel(
    tokens, meta, wg_in, wu_in, wd_in, out,
    wg, wu, wd, T, M, X, ZS, YR, PS, G, H, FAR, ADJ, FFR, FA, TRI,
    send, recv, local, wsem,
):
    where, ep, pep = neighbours()
    counter = [0]

    def remote(src, dst, to):
        index = counter[0]
        counter[0] += 1
        return pltpu.make_async_remote_copy(
            src_ref=src, dst_ref=dst, send_sem=send.at[index], recv_sem=recv.at[index],
            device_id=where[to], device_id_type=MESH,
        )

    loads = [
        pltpu.make_async_copy(src.at[e], dst.at[e], wsem.at[k, e])
        for e in range(2)
        for k, (src, dst) in enumerate(((wg_in, wg), (wu_in, wu), (wd_in, wd)))
    ]
    own = pltpu.make_async_copy(tokens, T.at[0, 0], local.at[0])
    own_meta = pltpu.make_async_copy(meta, M.at[0, 0, 0], local.at[1])
    own.start()
    own_meta.start()
    for load in loads:
        load.start()

    mz = remote(M.at[0, 0, 0], M.at[0, 0, 1], "z")
    mf = [
        remote(M.at[0, 0], M.at[0, 3], "a+"),
        remote(M.at[0, 0], M.at[0, 1], "a-"),
        remote(M.at[0, 3], M.at[0, 2], "a+"),
    ]
    ms = [
        remote(M.at[0], M.at[3], "b+"),
        remote(M.at[0], M.at[1], "b-"),
        remote(M.at[3], M.at[2], "b+"),
    ]
    f = {
        (3, 0): remote(T.at[0, 0, 0], T.at[0, 3, 0], "a+"),
        (3, 1): remote(T.at[0, 0, 1], T.at[0, 3, 1], "a+"),
        (2, 0): remote(T.at[0, 3, 0], T.at[0, 2, 0], "a+"),
        (1, 1): remote(T.at[0, 0, 1], T.at[0, 1, 1], "a-"),
        (1, 0): remote(T.at[0, 0, 0], T.at[0, 1, 0], "a-"),
        (2, 1): remote(T.at[0, 1, 1], T.at[0, 2, 1], "a-"),
    }
    s = {}
    for i in range(4):
        s[2, i, 0] = remote(T.at[0, i, 0], T.at[2, i, 0], "b+")
        s[2, i, 1] = remote(T.at[0, i, 1], T.at[2, i, 1], "b-")
        s[1, i, 0] = remote(T.at[2, i, 0], T.at[1, i, 0], "b+")
        s[1, i, 1] = remote(T.at[2, i, 1], T.at[1, i, 1], "b-")
        s[3, i, 1] = remote(T.at[0, i, 1], T.at[3, i, 1], "b+")
        s[3, i, 0] = remote(T.at[0, i, 0], T.at[3, i, 0], "b-")
    zs = {(c, i): remote(ZS.at[c, i], X.at[c, 1, i], "z") for c in range(4) for i in range(4)}
    zr = {(c, i): remote(X.at[c, 1, i], YR.at[c, i], "z") for c in range(4) for i in range(4)}
    far = {}
    adj = {}
    for i in range(4):
        far[i, 0] = remote(T.at[1, i, 0], FAR.at[i, 0], "b+")
        far[i, 1] = remote(T.at[1, i, 1], FAR.at[i, 1], "b-")
        adj[2, i, 0] = remote(T.at[2, i, 0], ADJ.at[1, i, 0], "b-")
        adj[2, i, 1] = remote(T.at[2, i, 1], ADJ.at[0, i, 1], "b+")
        adj[3, i, 0] = remote(T.at[3, i, 0], ADJ.at[0, i, 0], "b+")
        adj[3, i, 1] = remote(T.at[3, i, 1], ADJ.at[1, i, 1], "b-")
    ff = {
        0: remote(T.at[0, 2, 0], FFR.at[0], "a+"),
        1: remote(T.at[0, 2, 1], FFR.at[1], "a-"),
    }
    fa = {
        (1, 0): remote(T.at[0, 1, 0], FA.at[0, 0], "a+"),
        (1, 1): remote(T.at[0, 1, 1], FA.at[0, 1], "a+"),
        (3, 0): remote(T.at[0, 3, 0], FA.at[1, 0], "a-"),
        (3, 1): remote(T.at[0, 3, 1], FA.at[1, 1], "a-"),
    }

    barrier = pltpu.get_barrier_semaphore()
    for name in ("a+", "a-", "b+", "b-", "z"):
        pl.semaphore_signal(barrier, inc=1, device_id=where[name], device_id_type=MESH)

    lane = lax.broadcasted_iota(jnp.int32, (TOK, TOK), 1)
    row = lax.broadcasted_iota(jnp.int32, (TOK, TOK), 0)
    TRI[...] = jnp.where((row < lane) & ((row & 96) == (lane & 96)), 1.0, 0.0).astype(BF)
    own_meta.wait()
    own.wait()
    pl.semaphore_wait(barrier, 5)

    mz.start()
    f[3, 0].start()
    f[1, 1].start()
    s[2, 0, 0].start()
    s[2, 0, 1].start()
    f[3, 1].start()
    f[1, 0].start()

    sub8 = lax.broadcasted_iota(jnp.int32, (8, TOK), 0)
    lane8 = lax.broadcasted_iota(jnp.int32, (8, TOK), 1)
    sub32 = lax.broadcasted_iota(jnp.int32, (CAP, TOK), 0).astype(F32)
    expert = jnp.where(
        sub8 < 2, 2 * ep + sub8, jnp.where(sub8 < 4, 2 * pep + sub8 - 2, 2 * ep + sub8 - 4)
    )
    start_slot = ((lane8 & 96) >> 2).astype(F32)

    def pick(c, i, plane):
        if c == 0:
            return M[0, i, plane]
        if c == 1:
            return M[2, i, plane]
        low = lax.broadcasted_iota(jnp.int32, (16, TOK), 1) < HALF
        first, second = (3, 1) if c == 2 else (1, 3)
        return jnp.where(low, M[first, i, plane], M[second, i, plane])

    def pack(c, i):
        mine, theirs = pick(c, i, 0), pick(c, i, 1)
        member = jnp.zeros((8, TOK), F32)
        weight = jnp.zeros((8, TOK), jnp.int32)
        for k in range(8):
            ids = jnp.where(sub8 < 4, mine[k : k + 1], theirs[k : k + 1])
            nums = jnp.where(sub8 < 4, mine[8 + k : 9 + k], theirs[8 + k : 9 + k])
            hit = ids == expert
            member = member + jnp.where(hit, 1.0, 0.0)
            weight = weight + jnp.where(hit, nums, 0)
        before = jnp.dot(member.astype(BF), TRI[...], preferred_element_type=F32)
        code = jnp.where(member > 0.5, start_slot + before, -1.0)
        gate = weight.astype(F32) * (1.0 / 1024.0)
        hits = [sub32 == code[r : r + 1] for r in range(6)]
        places = jnp.concatenate([jnp.where(hits[r], 1.0, 0.0) for r in range(4)], axis=0).astype(BF)
        PS[c, i] = places
        for plane in range(2):
            for e in range(2):
                r = 4 * plane + e
                column = jnp.sum(jnp.where(hits[r], gate[r : r + 1], 0.0), axis=1, keepdims=True)
                G[c, e, plane, i] = jnp.broadcast_to(column, (CAP, TOK))
        for n in range(4):
            cols = slice(512 * n, 512 * n + 512)
            rows = T[c, i, :, :, cols].reshape(TOK, 512)
            packed = jnp.dot(places, rows, preferred_element_type=F32).astype(BF)
            X[c, 0, i, :, :, cols] = packed[:HALF].reshape(2, CAP, 512)
            ZS[c, i, :, :, cols] = packed[HALF:].reshape(2, CAP, 512)
        zs[c, i].start()

    def experts(c):
        for e in range(2):

            def gate_up(n, carry):
                cols = pl.ds(pl.multiple_of(n * 256, 256), 256)
                x = X[c, :, :, e].reshape(256, D)
                g = jnp.dot(x, wg[e, :, cols], preferred_element_type=F32)
                u = jnp.dot(x, wu[e, :, cols], preferred_element_type=F32)
                scale = G[c, e].reshape(256, TOK)[:, :1]
                H[:, cols] = (g / (1.0 + jnp.exp(-g)) * u * scale).astype(BF)
                return carry

            def down(n, carry):
                cols = pl.ds(pl.multiple_of(n * 512, 512), 512)
                y = jnp.dot(H[...], wd[e, :, cols], preferred_element_type=F32)
                X[c, :, :, e, :, cols] = y.astype(BF).reshape(2, 4, CAP, 512)
                return carry

            lax.fori_loop(0, 3, gate_up, 0)
            lax.fori_loop(0, 4, down, 0)

    def combine(c, i, extra, target=None):
        for n in range(4):
            cols = slice(512 * n, 512 * n + 512)
            y = jnp.concatenate(
                [X[c, 0, i, :, :, cols].reshape(HALF, 512), YR[c, i, :, :, cols].reshape(HALF, 512)], axis=0
            )
            total = lax.dot_general(PS[c, i], y, (((0,), (0,)), ((), ())), preferred_element_type=F32)
            for part in extra:
                total = total + part[:, :, cols].reshape(TOK, 512).astype(F32)
            if target is None:
                T[c, i, :, :, cols] = total.astype(BF).reshape(2, HALF, 512)
            else:
                target[:, cols] = total.astype(BF)

    mz.wait_recv()
    mf[0].start()
    mf[1].start()
    pack(0, 0)
    f[3, 0].wait_recv()
    f[2, 0].start()
    s[2, 3, 0].start()
    f[1, 1].wait_recv()
    f[2, 1].start()
    s[2, 1, 1].start()
    mf[0].wait_recv()
    mf[2].start()
    mf[1].wait_recv()
    f[1, 0].wait_recv()
    s[2, 1, 0].start()
    f[3, 1].wait_recv()
    s[2, 3, 1].start()
    mf[2].wait_recv()
    ms[0].start()
    ms[1].start()
    pack(0, 3)
    pack(0, 1)
    f[2, 0].wait_recv()
    s[2, 2, 0].start()
    f[2, 1].wait_recv()
    s[2, 2, 1].start()
    ms[0].wait_recv()
    ms[2].start()
    ms[1].wait_recv()
    pack(0, 2)
    for i in ORDER:
        s[2, i, 0].wait_recv()
        s[1, i, 0].start()
        s[2, i, 1].wait_recv()
        s[1, i, 1].start()
        pack(2, i)
    for i in ORDER:
        s[3, i, 1].start()
        s[3, i, 0].start()
    ms[2].wait_recv()

    for load in loads:
        load.wait()
    for i in ORDER:
        zs[0, i].wait_recv()
    experts(0)
    for i in ORDER:
        s[1, i, 0].wait_recv()
        s[1, i, 1].wait_recv()
        pack(1, i)
    for i in ORDER:
        zs[2, i].wait_recv()
    experts(2)
    for i in BACK:
        zr[2, i].start()
    for i in ORDER:
        s[3, i, 0].wait_recv()
        s[3, i, 1].wait_recv()
        pack(3, i)
    for i in ORDER:
        zs[1, i].wait_recv()
    experts(1)
    for i in BACK:
        zr[1, i].start()
    for copy in list(f.values()) + list(s.values()):
        copy.wait_send()
    for i in BACK:
        zr[2, i].wait_recv()
        combine(2, i, [])
        adj[2, i, 0].start()
        adj[2, i, 1].start()
    for i in ORDER:
        zs[3, i].wait_recv()
    experts(3)
    for i in BACK:
        zr[3, i].start()
    for i in BACK:
        zr[0, i].start()
    for i in BACK:
        zr[1, i].wait_recv()
        combine(1, i, [])
        far[i, 0].start()
        far[i, 1].start()
    for i in BACK:
        zr[3, i].wait_recv()
        far[i, 0].wait_recv()
        far[i, 1].wait_recv()
        combine(3, i, [FAR.at[i]])
        adj[3, i, 0].start()
        adj[3, i, 1].start()
    for i in BACK:
        zr[0, i].wait_recv()
        for c in (2, 3):
            adj[c, i, 0].wait_recv()
            adj[c, i, 1].wait_recv()
        if i:
            combine(0, i, [ADJ.at[0, i], ADJ.at[1, i]])
        if i == 2:
            ff[0].start()
            ff[1].start()
        if i == 1:
            fa[1, 1].start()
            ff[0].wait_recv()
            T[0, 1, 0] = (T[0, 1, 0].astype(F32) + FFR[0].astype(F32)).astype(BF)
            fa[1, 0].start()
        if i == 3:
            fa[3, 0].start()
            ff[1].wait_recv()
            T[0, 3, 1] = (T[0, 3, 1].astype(F32) + FFR[1].astype(F32)).astype(BF)
            fa[3, 1].start()
    for copy in fa.values():
        copy.wait_recv()
    combine(0, 0, [ADJ.at[0, 0], ADJ.at[1, 0], FA.at[0], FA.at[1]], out)

    for copy in [mz, *mf, *ms, *zs.values(), *zr.values(), *far.values(), *adj.values(), *ff.values(), *fa.values()]:
        copy.wait_send()


COPIES = 7 + 6 + 24 + 16 + 16 + 8 + 16 + 2 + 4


def shards(tokens, expert_ids, gate_nums, w_gate, w_up, w_down):
    meta = jnp.concatenate([expert_ids.T, gate_nums.T], axis=0)
    anywhere = pl.BlockSpec(memory_space=pl.ANY)
    return pl.pallas_call(
        kernel,
        name="routed_experts",
        out_shape=jax.ShapeDtypeStruct((TOK, D), BF),
        in_specs=[anywhere] * 5,
        out_specs=pl.BlockSpec(memory_space=pltpu.VMEM),
        scratch_shapes=[
            pltpu.VMEM((2, D, FF), BF),
            pltpu.VMEM((2, D, FF), BF),
            pltpu.VMEM((2, FF, D), BF),
            pltpu.VMEM((4, 4, 2, HALF, D), BF),
            pltpu.VMEM((4, 4, 2, 16, TOK), jnp.int32),
            pltpu.VMEM((4, 2, 4, 2, CAP, D), BF),
            pltpu.VMEM((4, 4, 2, CAP, D), BF),
            pltpu.VMEM((4, 4, 2, CAP, D), BF),
            pltpu.VMEM((4, 4, TOK, TOK), BF),
            pltpu.VMEM((4, 2, 2, 4, CAP, TOK), F32),
            pltpu.VMEM((256, FF), BF),
            pltpu.VMEM((4, 2, HALF, D), BF),
            pltpu.VMEM((2, 4, 2, HALF, D), BF),
            pltpu.VMEM((2, HALF, D), BF),
            pltpu.VMEM((2, 2, HALF, D), BF),
            pltpu.VMEM((TOK, TOK), BF),
            pltpu.SemaphoreType.DMA((COPIES,)),
            pltpu.SemaphoreType.DMA((COPIES,)),
            pltpu.SemaphoreType.DMA((2,)),
            pltpu.SemaphoreType.DMA((3, 2)),
        ],
        compiler_params=pltpu.CompilerParams(
            collective_id=0, has_side_effects=True, vmem_limit_bytes=67043328
        ),
    )(tokens.reshape(2, HALF, D), meta, w_gate, w_up, w_down)


def solution(mesh):
    placed = (
        P(("dp", "ep"), None),
        P(("dp", "ep"), None),
        P(("dp", "ep"), None),
        P("ep", None, None),
        P("ep", None, None),
        P("ep", None, None),
    )
    return jax.shard_map(
        shards, mesh=mesh, in_specs=placed, out_specs=P(("dp", "ep"), None), check_vma=False
    )
```

profile of v0, /device:TPU:70, one launch (start us, length us, event | category | flops | bytes accessed | tf_op | source)
XLA Modules:
  0.0 137.0 jit_solution(12956101112143645129)
XLA Ops:
  0.0 1.3 pad_add_fusion.meta
  1.3 133.8 %routed_experts.1 = bf16[128,2048]{1,0:T(8,128)(2,1)} custom-call(bf16[2,64,2048]{2,1,0:T(8,128)(2,1)} %bitcast.3, s32[16,128]{1,0:T(8,128)} %pad_add_fusion.meta, bf16[2,2048,768]{2,1,0:T(8,128)(2,1)} %wg_in.1, bf16[2,2048,768]{2,1,0:T(8,128)(2,1)} %wu_in.1, bf16[2,768,2048]{2,1,0:T(8,128)(2,1)} %wd_in.1), custom_call_target="tpu_custom_call" | custom-call | tf_op jit(solution)/shard_map/routed_experts/pallas_call | solution.py:347
  135.1 1.9 %copy.8 = bf16[128,2048]{1,0:T(8,128)(2,1)} copy(bf16[128,2048]{1,0:T(8,128)(2,1)} %routed_experts.1) | data formatting | bytes 1048576
where the time goes:
time: 137 us
  Pallas kernels  134 us (98%)
  local copies, waits for them, and re-layouts  1.88 us (1%)
    pallas_call x1, Pallas kernels, shards(): pl.pallas_call(kernel, name='routed_experts', out_shape=jax.ShapeDtypeStr...  134 us

commit v1 on v0

v1 whole, which is shorter than its diff:
```python
import jax
import jax.numpy as jnp
from jax import lax
from jax.experimental import pallas as pl
from jax.experimental.pallas import tpu as pltpu
from jax.sharding import PartitionSpec as P

MESH = pl.DeviceIdType.MESH
BF = jnp.bfloat16
F32 = jnp.float32
D = 2048
FF = 768
TOK = 128
HALF = 64
CAP = 32
ORDER = (0, 3, 1, 2)
BACK = (2, 3, 1, 0)


def neighbours():
    dp, ep = lax.axis_index("dp"), lax.axis_index("ep")
    z_hi, core = dp // 2, dp % 2
    x, z_lo, y = ep // 8, (ep // 4) % 2, ep % 4
    z = z_hi * 2 + z_lo
    a = (1 - core) * x + core * y
    b = (1 - core) * y + core * x

    def device(a, b, z):
        px = (1 - core) * a + core * b
        py = (1 - core) * b + core * a
        return ((z // 2) * 2 + core, (px * 2 + z % 2) * 4 + py)

    up = z + 1 - 2 * (z % 2)
    down = (z + 3 + 2 * (z % 2)) % 4
    zp = (1 - core) * up + core * down
    where = {
        "a+": device((a + 1) % 4, b, z),
        "a-": device((a + 3) % 4, b, z),
        "a2": device((a + 2) % 4, b, z),
        "b2": device(a, (b + 2) % 4, z),
        "b+": device(a, (b + 1) % 4, z),
        "b-": device(a, (b + 3) % 4, z),
        "z": device(a, b, zp),
    }
    return where, ep, where["z"][1]


def kernel(
    tokens, ids_in, nums_in, wg_in, wu_in, wd_in, out,
    wg, wu, wd, IN, T, M, X, ZS, YR, PS, G, H, FAR, ADJ, FFR, FA, TRI,
    send, recv, local, wsem,
):
    where, ep, pep = neighbours()
    counter = [0]

    def remote(src, dst, to):
        index = counter[0]
        counter[0] += 1
        return pltpu.make_async_remote_copy(
            src_ref=src, dst_ref=dst, send_sem=send.at[index], recv_sem=recv.at[index],
            device_id=where[to], device_id_type=MESH,
        )

    loads = [
        pltpu.make_async_copy(src.at[e], dst.at[e], wsem.at[k, e])
        for e in range(2)
        for k, (src, dst) in enumerate(((wg_in, wg), (wu_in, wu), (wd_in, wd)))
    ]
    own = pltpu.make_async_copy(tokens, T.at[0, 0], local.at[0])
    tables = [
        pltpu.make_async_copy(ids_in, IN.at[0], local.at[1]),
        pltpu.make_async_copy(nums_in, IN.at[1], local.at[2]),
    ]
    own.start()
    for table in tables:
        table.start()

    mf = [
        remote(M.at[0, 0, 0], M.at[0, 0, 3], "a+"),
        remote(M.at[0, 0, 0], M.at[0, 0, 1], "a-"),
        remote(M.at[0, 0, 0], M.at[0, 0, 2], "a2"),
    ]
    ms = {
        3: remote(M.at[0, 0], M.at[0, 3], "b+"),
        1: remote(M.at[0, 0], M.at[0, 1], "b-"),
        2: remote(M.at[0, 0], M.at[0, 2], "b2"),
    }
    mz = [remote(M.at[0, j], M.at[1, j], "z") for j in range(4)]
    f = {
        (3, 0): remote(T.at[0, 0, 0], T.at[0, 3, 0], "a+"),
        (1, 1): remote(T.at[0, 0, 1], T.at[0, 1, 1], "a+"),
        (2, 0): remote(T.at[0, 3, 0], T.at[0, 2, 0], "a+"),
        (3, 1): remote(T.at[0, 0, 1], T.at[0, 3, 1], "a-"),
        (1, 0): remote(T.at[0, 0, 0], T.at[0, 1, 0], "a-"),
        (2, 1): remote(T.at[0, 3, 1], T.at[0, 2, 1], "a-"),
    }
    s = {}
    for i in range(4):
        s[2, i, 0] = remote(T.at[0, i, 0], T.at[2, i, 0], "b+")
        s[2, i, 1] = remote(T.at[0, i, 1], T.at[2, i, 1], "b-")
        s[1, i, 0] = remote(T.at[2, i, 0], T.at[1, i, 0], "b+")
        s[1, i, 1] = remote(T.at[2, i, 1], T.at[1, i, 1], "b-")
        s[3, i, 1] = remote(T.at[0, i, 1], T.at[3, i, 1], "b+")
        s[3, i, 0] = remote(T.at[0, i, 0], T.at[3, i, 0], "b-")
    zs = {(c, i): remote(ZS.at[c, i], X.at[c, 1, i], "z") for c in range(4) for i in range(4)}
    zr = {(c, i): remote(X.at[c, 1, i], YR.at[c, i], "z") for c in range(4) for i in range(4)}
    far = {}
    adj = {}
    for i in range(4):
        far[i, 0] = remote(T.at[1, i, 0], FAR.at[i, 0], "b+")
        far[i, 1] = remote(T.at[1, i, 1], FAR.at[i, 1], "b-")
        adj[2, i, 0] = remote(T.at[2, i, 0], ADJ.at[1, i, 0], "b-")
        adj[2, i, 1] = remote(T.at[2, i, 1], ADJ.at[0, i, 1], "b+")
        adj[3, i, 0] = remote(T.at[3, i, 0], ADJ.at[0, i, 0], "b+")
        adj[3, i, 1] = remote(T.at[3, i, 1], ADJ.at[1, i, 1], "b-")
    ff = {
        0: remote(T.at[0, 2, 0], FFR.at[0], "a+"),
        1: remote(T.at[0, 2, 1], FFR.at[1], "a-"),
    }
    fa = {
        (1, 0): remote(T.at[0, 1, 0], FA.at[0, 0], "a+"),
        (3, 1): remote(T.at[0, 3, 1], FA.at[0, 1], "a+"),
        (3, 0): remote(T.at[0, 3, 0], FA.at[1, 0], "a-"),
        (1, 1): remote(T.at[0, 1, 1], FA.at[1, 1], "a-"),
    }

    barrier = pltpu.get_barrier_semaphore()
    peers = ("a+", "a-", "a2", "b+", "b-", "b2", "z")
    for name in peers:
        pl.semaphore_signal(barrier, inc=1, device_id=where[name], device_id_type=MESH)

    lane = lax.broadcasted_iota(jnp.int32, (TOK, TOK), 1)
    row = lax.broadcasted_iota(jnp.int32, (TOK, TOK), 0)
    TRI[...] = jnp.where((row < lane) & ((row & 96) == (lane & 96)), 1.0, 0.0).astype(BF)
    for k, table in enumerate(tables):
        table.wait()
        M[0, 0, 0, 8 * k : 8 * k + 8] = jnp.transpose(IN[k].astype(F32)).astype(jnp.int32)
    own.wait()
    for load in loads:
        load.start()

    sub8 = lax.broadcasted_iota(jnp.int32, (8, TOK), 0)
    lane8 = lax.broadcasted_iota(jnp.int32, (8, TOK), 1)
    sub32 = lax.broadcasted_iota(jnp.int32, (CAP, TOK), 0).astype(F32)
    expert = jnp.where(sub8 < 2, 2 * ep + sub8, 2 * pep + sub8 - 2)
    start_slot = ((lane8 & 96) >> 2).astype(F32)

    low = lax.broadcasted_iota(jnp.int32, (16, TOK), 1) < HALF

    def pick(c, i, plane):
        first, second = ((0, 0), (2, 2), (3, 1), (1, 3))[c]
        return jnp.where(low, M[plane, first, i], M[plane, second, (4 - i) % 4])

    def slots_of(table):
        member = jnp.zeros((8, TOK), F32)
        weight = jnp.zeros((8, TOK), jnp.int32)
        for k in range(8):
            hit = table[k : k + 1] == expert
            member = member + jnp.where(hit, 1.0, 0.0)
            weight = weight + jnp.where(hit, table[8 + k : 9 + k], 0)
        before = jnp.dot(member.astype(BF), TRI[...], preferred_element_type=F32)
        code = jnp.where(member > 0.5, start_slot + before, -1.0)
        return code, weight.astype(F32) * (1.0 / 1024.0)

    def weigh(c, i, plane, hits, gate):
        for e in range(2):
            column = jnp.sum(jnp.where(hits[e], gate[e : e + 1], 0.0), axis=1, keepdims=True)
            G[c, e, plane, i] = jnp.broadcast_to(column, (CAP, TOK))

    def pack(c, i):
        code, gate = slots_of(pick(c, i, 0))
        hits = [sub32 == code[r : r + 1] for r in range(4)]
        places = jnp.concatenate([jnp.where(hits[r], 1.0, 0.0) for r in range(4)], axis=0).astype(BF)
        PS[c, i] = places
        for n in range(4):
            cols = slice(512 * n, 512 * n + 512)
            rows = T[c, i, :, :, cols].reshape(TOK, 512)
            packed = jnp.dot(places, rows, preferred_element_type=F32).astype(BF)
            X[c, 0, i, :, :, cols] = packed[:HALF].reshape(2, CAP, 512)
            ZS[c, i, :, :, cols] = packed[HALF:].reshape(2, CAP, 512)
        weigh(c, i, 0, hits, gate)

    def weigh_theirs(c):
        for i in range(4):
            code, gate = slots_of(pick(c, i, 1))
            weigh(c, i, 1, [sub32 == code[r : r + 1] for r in range(2)], gate)

    def gate_up(c, e):
        def step(n, carry):
            cols = pl.ds(pl.multiple_of(n * 256, 256), 256)
            x = X[c, :, :, e].reshape(256, D)
            g = jnp.dot(x, wg[e, :, cols], preferred_element_type=F32)
            u = jnp.dot(x, wu[e, :, cols], preferred_element_type=F32)
            scale = G[c, e].reshape(256, TOK)[:, :1]
            H[:, cols] = (g / (1.0 + jnp.exp(-g)) * u * scale).astype(BF)
            return carry

        lax.fori_loop(0, 3, step, 0)

    def down(c, e):
        def step(n, carry):
            cols = pl.ds(pl.multiple_of(n * 512, 512), 512)
            y = jnp.dot(H[...], wd[e, :, cols], preferred_element_type=F32)
            X[c, :, :, e, :, cols] = y.astype(BF).reshape(2, 4, CAP, 512)
            return carry

        lax.fori_loop(0, 4, step, 0)

    def experts(c, between):
        if c != 3:
            for i in ORDER:
                zs[c, i].wait_recv()
        weigh_theirs(c)
        between = list(between)
        for e in range(2):
            gate_up(c, e)
            if between:
                between.pop(0)()
            down(c, e)
            if between:
                between.pop(0)()
        for task in between:
            task()

    def combine(c, i, extra, target=None):
        for n in range(4):
            cols = slice(512 * n, 512 * n + 512)
            y = jnp.concatenate(
                [X[c, 0, i, :, :, cols].reshape(HALF, 512), YR[c, i, :, :, cols].reshape(HALF, 512)], axis=0
            )
            total = lax.dot_general(PS[c, i], y, (((0,), (0,)), ((), ())), preferred_element_type=F32)
            for part in extra:
                total = total + part[:, :, cols].reshape(TOK, 512).astype(F32)
            if target is None:
                T[c, i, :, :, cols] = total.astype(BF).reshape(2, HALF, 512)
            else:
                target[:, cols] = total.astype(BF)

    def pack_send(c, i):
        pack(c, i)
        zs[c, i].start()

    def near(i):
        for h in range(2):
            s[2, i, h].wait_recv()
            s[1, i, h].start()
        pack_send(2, i)

    def others(i):
        s[3, i, 1].start()
        s[3, i, 0].start()

    def distant(c, i):
        s[c, i, 0].wait_recv()
        s[c, i, 1].wait_recv()
        pack_send(c, i)

    pack(0, 0)
    pl.semaphore_wait(barrier, len(peers))
    for copy in mf:
        copy.start()
    zs[0, 0].start()
    for key in ((3, 0), (3, 1), (1, 1), (1, 0)):
        f[key].start()
    for copy in mf:
        copy.wait_recv()
    for j in (1, 3, 2):
        ms[j].start()
    f[3, 0].wait_recv()
    f[2, 0].start()
    f[3, 1].wait_recv()
    f[2, 1].start()
    pack_send(0, 3)
    mz[0].start()
    for i in (0, 3):
        s[2, i, 0].start()
        s[2, i, 1].start()
    f[1, 0].wait_recv()
    f[1, 1].wait_recv()
    pack_send(0, 1)
    s[2, 1, 0].start()
    s[2, 1, 1].start()
    f[2, 0].wait_recv()
    f[2, 1].wait_recv()
    pack_send(0, 2)
    s[2, 2, 0].start()
    s[2, 2, 1].start()
    for j in (1, 3, 2):
        ms[j].wait_recv()
        mz[j].start()
    near(0)
    near(3)
    others(0)
    near(1)
    others(3)
    for copy in mz:
        copy.wait_recv()
    for load in loads:
        load.wait()

    def last_near():
        near(2)
        others(1)
        others(2)

    experts(0, [last_near])
    distant(1, 0)
    distant(1, 3)
    experts(2, [lambda c=c, i=i: distant(c, i) for c, i in ((1, 1), (1, 2), (3, 0), (3, 3))])
    distant(3, 1)
    distant(3, 2)
    for i in BACK:
        zr[2, i].start()

    def returned(c, i):
        zr[c, i].wait_recv()
        extra = []
        if c == 3:
            far[i, 0].wait_recv()
            far[i, 1].wait_recv()
            extra = [FAR.at[i]]
        combine(c, i, extra)
        for h in range(2):
            (far[i, h] if c == 1 else adj[c, i, h]).start()

    for copy in list(f.values()) + list(s.values()):
        copy.wait_send()
    experts(1, [])
    for i, k in zip(ORDER, BACK):
        zs[3, i].wait_recv()
        zr[1, k].start()
    returned(2, BACK[0])
    returned(2, BACK[1])
    experts(3, [lambda i=i: returned(2, i) for i in BACK[2:]])
    for i in BACK:
        zr[3, i].start()
    for i in BACK:
        returned(1, i)
    for i in BACK:
        returned(3, i)
        zr[0, i].start()
    for i in BACK:
        zr[0, i].wait_recv()
        for c in (2, 3):
            adj[c, i, 0].wait_recv()
            adj[c, i, 1].wait_recv()
        extra = [ADJ.at[0, i], ADJ.at[1, i]]
        if i == 2:
            combine(0, 2, extra)
            ff[0].start()
            ff[1].start()
        if i == 3:
            combine(0, 3, extra)
            fa[3, 0].start()
            fa[3, 1].start()
        if i == 1:
            ff[0].wait_recv()
            ff[1].wait_recv()
            combine(0, 1, extra + [FFR])
            fa[1, 0].start()
            fa[1, 1].start()
        if i == 0:
            for copy in fa.values():
                copy.wait_recv()
            combine(0, 0, extra + [FA.at[0], FA.at[1]], out)

    for copy in [*mz, *mf, *ms.values(), *zs.values(), *zr.values(), *far.values(), *adj.values(), *ff.values(), *fa.values()]:
        copy.wait_send()


COPIES = 10 + 6 + 24 + 16 + 16 + 8 + 16 + 2 + 4


def shards(tokens, expert_ids, gate_nums, w_gate, w_up, w_down):
    anywhere = pl.BlockSpec(memory_space=pl.ANY)
    return pl.pallas_call(
        kernel,
        name="routed_experts",
        out_shape=jax.ShapeDtypeStruct((TOK, D), BF),
        in_specs=[anywhere] * 6,
        out_specs=pl.BlockSpec(memory_space=pltpu.VMEM),
        scratch_shapes=[
            pltpu.VMEM((2, D, FF), BF),
            pltpu.VMEM((2, D, FF), BF),
            pltpu.VMEM((2, FF, D), BF),
            pltpu.VMEM((2, TOK, 8), jnp.int32),
            pltpu.VMEM((4, 4, 2, HALF, D), BF),
            pltpu.VMEM((2, 4, 4, 16, TOK), jnp.int32),
            pltpu.VMEM((4, 2, 4, 2, CAP, D), BF),
            pltpu.VMEM((4, 4, 2, CAP, D), BF),
            pltpu.VMEM((4, 4, 2, CAP, D), BF),
            pltpu.VMEM((4, 4, TOK, TOK), BF),
            pltpu.VMEM((4, 2, 2, 4, CAP, TOK), F32),
            pltpu.VMEM((256, FF), BF),
            pltpu.VMEM((4, 2, HALF, D), BF),
            pltpu.VMEM((2, 4, 2, HALF, D), BF),
            pltpu.VMEM((2, HALF, D), BF),
            pltpu.VMEM((2, 2, HALF, D), BF),
            pltpu.VMEM((TOK, TOK), BF),
            pltpu.SemaphoreType.DMA((COPIES,)),
            pltpu.SemaphoreType.DMA((COPIES,)),
            pltpu.SemaphoreType.DMA((3,)),
            pltpu.SemaphoreType.DMA((3, 2)),
        ],
        compiler_params=pltpu.CompilerParams(
            collective_id=0, has_side_effects=True, vmem_limit_bytes=67043328
        ),
    )(tokens.reshape(2, HALF, D), expert_ids, gate_nums, w_gate, w_up, w_down)


def solution(mesh):
    placed = (
        P(("dp", "ep"), None),
        P(("dp", "ep"), None),
        P(("dp", "ep"), None),
        P("ep", None, None),
        P("ep", None, None),
        P("ep", None, None),
    )
    return jax.shard_map(
        shards, mesh=mesh, in_specs=placed, out_specs=P(("dp", "ep"), None), check_vma=False
    )
```

time: 137 us -> 123 us (0.90)
  the two profiles are of different devices: /device:TPU:70 before, /device:TPU:0 now
where the time goes in v1:
time: 123 us
  Pallas kernels  118 us (96%)
  local copies, waits for them, and re-layouts  4.7 us (4%)
    pallas_call x1, Pallas kernels, shards(): pl.pallas_call(kernel, name='routed_experts', out_shape=jax.ShapeDtypeStr...  118 us
    unnamed x3, local copies, waits for them, and re-layouts  4.7 us

profile of v1, /device:TPU:0, one launch (start us, length us, event | category | flops | bytes accessed | tf_op | source)
XLA Modules:
  0.0 122.5 jit_solution(15005611030246798841)
XLA Ops:
  0.0 1.4 %copy.7.ids_in = s32[128,8]{1,0:T(8,128)} copy(s32[128,8]{0,1:T(8,128)} %param.7) | data formatting | bytes 8192 | tf_op args[1]
  1.4 1.4 %copy.8.nums_in = s32[128,8]{1,0:T(8,128)} copy(s32[128,8]{0,1:T(8,128)} %param.8) | data formatting | bytes 8192 | tf_op args[2]
  2.8 117.8 %routed_experts.1 = bf16[128,2048]{1,0:T(8,128)(2,1)} custom-call(bf16[2,64,2048]{2,1,0:T(8,128)(2,1)} %bitcast.1, s32[128,8]{1,0:T(8,128)} %copy.7.ids_in, s32[128,8]{1,0:T(8,128)} %copy.8.nums_in, bf16[2,2048,768]{2,1,0:T(8,128)(2,1)} %wg_in.1, bf16[2,2048,768]{2,1,0:T(8,128)(2,1)} %wu_in.1, bf16[2,768,2048]{2,1,0:T(8,128)(2,1)} %wd_in.1), custom_call_target="tpu_custom_call" | custom-call | tf_op jit(solution)/shard_map/routed_experts/pallas_call | solution.py:376
  120.6 1.9 %copy.10 = bf16[128,2048]{1,0:T(8,128)(2,1)} copy(bf16[128,2048]{1,0:T(8,128)(2,1)} %routed_experts.1) | data formatting | bytes 1048576

commit v2 on v1

--- a/solution.py
+++ b/solution.py
@@ -47,7 +47,7 @@
 
 def kernel(
     tokens, ids_in, nums_in, wg_in, wu_in, wd_in, out,
-    wg, wu, wd, IN, T, M, X, ZS, YR, PS, G, H, FAR, ADJ, FFR, FA, TRI,
+    wg, wu, wd, T, M, X, ZS, YR, PS, G, H, FAR, ADJ, FFR, FA, TRI,
     send, recv, local, wsem,
 ):
     where, ep, pep = neighbours()
@@ -68,8 +68,8 @@
     ]
     own = pltpu.make_async_copy(tokens, T.at[0, 0], local.at[0])
     tables = [
-        pltpu.make_async_copy(ids_in, IN.at[0], local.at[1]),
-        pltpu.make_async_copy(nums_in, IN.at[1], local.at[2]),
+        pltpu.make_async_copy(ids_in, M.at[0, 0, 0, pl.ds(0, 8)], local.at[1]),
+        pltpu.make_async_copy(nums_in, M.at[0, 0, 0, pl.ds(8, 8)], local.at[2]),
     ]
     own.start()
     for table in tables:
@@ -132,9 +132,8 @@
     lane = lax.broadcasted_iota(jnp.int32, (TOK, TOK), 1)
     row = lax.broadcasted_iota(jnp.int32, (TOK, TOK), 0)
     TRI[...] = jnp.where((row < lane) & ((row & 96) == (lane & 96)), 1.0, 0.0).astype(BF)
-    for k, table in enumerate(tables):
+    for table in tables:
         table.wait()
-        M[0, 0, 0, 8 * k : 8 * k + 8] = jnp.transpose(IN[k].astype(F32)).astype(jnp.int32)
     own.wait()
     for load in loads:
         load.start()
@@ -185,42 +184,45 @@
             code, gate = slots_of(pick(c, i, 1))
             weigh(c, i, 1, [sub32 == code[r : r + 1] for r in range(2)], gate)
 
-    def gate_up(c, e):
-        def step(n, carry):
-            cols = pl.ds(pl.multiple_of(n * 256, 256), 256)
-            x = X[c, :, :, e].reshape(256, D)
-            g = jnp.dot(x, wg[e, :, cols], preferred_element_type=F32)
-            u = jnp.dot(x, wu[e, :, cols], preferred_element_type=F32)
-            scale = G[c, e].reshape(256, TOK)[:, :1]
-            H[:, cols] = (g / (1.0 + jnp.exp(-g)) * u * scale).astype(BF)
+    def gate_up(c, e, n):
+        cols = slice(256 * n, 256 * n + 256) if isinstance(n, int) else pl.ds(pl.multiple_of(n * 256, 256), 256)
+        x = X[c, :, :, e].reshape(256, D)
+        g = jnp.dot(x, wg[e, :, cols], preferred_element_type=F32)
+        u = jnp.dot(x, wu[e, :, cols], preferred_element_type=F32)
+        scale = G[c, e].reshape(256, TOK)[:, :1]
+        H[:, cols] = (g / (1.0 + jnp.exp(-g)) * u * scale).astype(BF)
+
+    def down(c, e, n):
+        cols = pl.ds(pl.multiple_of(n * 512, 512), 512)
+        y = jnp.dot(H[...], wd[e, :, cols], preferred_element_type=F32)
+        X[c, :, :, e, :, cols] = y.astype(BF).reshape(2, 4, CAP, 512)
+
+    def loop(low, high, step):
+        def body(n, carry):
+            step(n)
             return carry
 
-        lax.fori_loop(0, 3, step, 0)
-
-    def down(c, e):
-        def step(n, carry):
-            cols = pl.ds(pl.multiple_of(n * 512, 512), 512)
-            y = jnp.dot(H[...], wd[e, :, cols], preferred_element_type=F32)
-            X[c, :, :, e, :, cols] = y.astype(BF).reshape(2, 4, CAP, 512)
-            return carry
-
-        lax.fori_loop(0, 4, step, 0)
-
-    def experts(c, between):
-        if c != 3:
-            for i in ORDER:
-                zs[c, i].wait_recv()
+        lax.fori_loop(low, high, body, 0)
+
+    def arrived(c):
+        for i in ORDER:
+            zs[c, i].wait_recv()
         weigh_theirs(c)
-        between = list(between)
-        for e in range(2):
-            gate_up(c, e)
-            if between:
-                between.pop(0)()
-            down(c, e)
-            if between:
-                between.pop(0)()
-        for task in between:
-            task()
+
+    def fine(c, e):
+        return [lambda n=n: gate_up(c, e, n) for n in range(3)] + [
+            lambda n=n: loop(n, n + 2, lambda m: down(c, e, m)) for n in (0, 2)
+        ]
+
+    def coarse(c, e):
+        return [
+            lambda: loop(0, 3, lambda n: gate_up(c, e, n)),
+            lambda: loop(0, 4, lambda m: down(c, e, m)),
+        ]
+
+    def run(steps, count=None):
+        for _ in range(len(steps) if count is None else count):
+            steps.pop(0)()
 
     def combine(c, i, extra, target=None):
         for n in range(4):
@@ -255,31 +257,61 @@
         s[c, i, 1].wait_recv()
         pack_send(c, i)
 
+    def returned(c, i):
+        zr[c, i].wait_recv()
+        extra = []
+        if c == 3:
+            far[i, 0].wait_recv()
+            far[i, 1].wait_recv()
+            extra = [FAR.at[i]]
+        combine(c, i, extra)
+        for h in range(2):
+            (far[i, h] if c == 1 else adj[c, i, h]).start()
+
+    def pack_send(c, i):
+        pack(c, i)
+        zs[c, i].start()
+
+    def near(i):
+        for h in range(2):
+            s[2, i, h].wait_recv()
+            s[1, i, h].start()
+        pack_send(2, i)
+
+    def others(i):
+        s[3, i, 1].start()
+        s[3, i, 0].start()
+
+    def distant(c, i):
+        s[c, i, 0].wait_recv()
+        s[c, i, 1].wait_recv()
+        pack_send(c, i)
+
     pack(0, 0)
     pl.semaphore_wait(barrier, len(peers))
+    f[3, 0].start()
+    f[3, 1].start()
     for copy in mf:
         copy.start()
     zs[0, 0].start()
-    for key in ((3, 0), (3, 1), (1, 1), (1, 0)):
-        f[key].start()
+    f[1, 1].start()
+    f[1, 0].start()
+    f[3, 0].wait_recv()
+    f[2, 0].start()
+    f[3, 1].wait_recv()
+    f[2, 1].start()
     for copy in mf:
         copy.wait_recv()
     for j in (1, 3, 2):
         ms[j].start()
-    f[3, 0].wait_recv()
-    f[2, 0].start()
-    f[3, 1].wait_recv()
-    f[2, 1].start()
     pack_send(0, 3)
     mz[0].start()
-    for i in (0, 3):
+    f[1, 0].wait_recv()
+    f[1, 1].wait_recv()
+    for i in (0, 3, 1):
         s[2, i, 0].start()
         s[2, i, 1].start()
-    f[1, 0].wait_recv()
-    f[1, 1].wait_recv()
     pack_send(0, 1)
-    s[2, 1, 0].start()
-    s[2, 1, 1].start()
     f[2, 0].wait_recv()
     f[2, 1].wait_recv()
     pack_send(0, 2)
@@ -293,76 +325,93 @@
     others(0)
     near(1)
     others(3)
+    near(2)
+    others(1)
+    others(2)
+    distant(1, 0)
     for copy in mz:
         copy.wait_recv()
     for load in loads:
         load.wait()
-
-    def last_near():
-        near(2)
-        others(1)
-        others(2)
-
-    experts(0, [last_near])
-    distant(1, 0)
+    arrived(0)
+    first = fine(0, 0)
+    run(first, 2)
     distant(1, 3)
-    experts(2, [lambda c=c, i=i: distant(c, i) for c, i in ((1, 1), (1, 2), (3, 0), (3, 3))])
+    run(first, 2)
+    distant(3, 0)
+    run(first)
+    distant(1, 1)
+    arrived(2)
+    second = fine(2, 0) + fine(2, 1)
+    run(second, 2)
+    distant(3, 3)
+    run(second, 3)
+    distant(1, 2)
+    run(second, 2)
     distant(3, 1)
+    run(second, 2)
     distant(3, 2)
+    run(second)
     for i in BACK:
         zr[2, i].start()
-
-    def returned(c, i):
-        zr[c, i].wait_recv()
-        extra = []
-        if c == 3:
-            far[i, 0].wait_recv()
-            far[i, 1].wait_recv()
-            extra = [FAR.at[i]]
-        combine(c, i, extra)
-        for h in range(2):
-            (far[i, h] if c == 1 else adj[c, i, h]).start()
-
     for copy in list(f.values()) + list(s.values()):
         copy.wait_send()
-    experts(1, [])
+    arrived(1)
+    run(coarse(1, 0) + coarse(1, 1))
     for i, k in zip(ORDER, BACK):
         zs[3, i].wait_recv()
         zr[1, k].start()
-    returned(2, BACK[0])
-    returned(2, BACK[1])
-    experts(3, [lambda i=i: returned(2, i) for i in BACK[2:]])
-    for i in BACK:
-        zr[3, i].start()
-    for i in BACK:
-        returned(1, i)
-    for i in BACK:
-        returned(3, i)
-        zr[0, i].start()
-    for i in BACK:
+    weigh_theirs(3)
+    returned(2, 2)
+    third = coarse(3, 0) + coarse(3, 1)
+    run(third, 1)
+    returned(2, 3)
+    run(third, 1)
+    returned(2, 1)
+    run(third, 1)
+    returned(2, 0)
+    run(third)
+    zr[3, 2].start()
+    zr[3, 3].start()
+    returned(1, 2)
+    last = coarse(0, 1)
+    run(last, 1)
+    returned(1, 3)
+    run(last)
+    returned(1, 1)
+    returned(1, 0)
+    zr[0, 2].start()
+    zr[3, 1].start()
+
+    def finish(i, extra, target=None):
         zr[0, i].wait_recv()
         for c in (2, 3):
             adj[c, i, 0].wait_recv()
             adj[c, i, 1].wait_recv()
-        extra = [ADJ.at[0, i], ADJ.at[1, i]]
-        if i == 2:
-            combine(0, 2, extra)
-            ff[0].start()
-            ff[1].start()
-        if i == 3:
-            combine(0, 3, extra)
-            fa[3, 0].start()
-            fa[3, 1].start()
-        if i == 1:
-            ff[0].wait_recv()
-            ff[1].wait_recv()
-            combine(0, 1, extra + [FFR])
-            fa[1, 0].start()
-            fa[1, 1].start()
-        if i == 0:
-            for copy in fa.values():
-                copy.wait_recv()
-            combine(0, 0, extra + [FA.at[0], FA.at[1]], out)
+        combine(0, i, [ADJ.at[0, i], ADJ.at[1, i]] + extra, target)
+
+    returned(3, 2)
+    zr[0, 3].start()
+    returned(3, 3)
+    zr[3, 0].start()
+    finish(2, [])
+    ff[0].start()
+    ff[1].start()
+    zr[0, 1].start()
+    returned(3, 1)
+    zr[0, 0].start()
+    finish(3, [])
+    fa[3, 0].start()
+    fa[3, 1].start()
+    returned(3, 0)
+    ff[0].wait_recv()
+    ff[1].wait_recv()
+    finish(1, [FFR])
+    fa[1, 0].start()
+    fa[1, 1].start()
+    for copy in fa.values():
+        copy.wait_recv()
+    finish(0, [FA.at[0], FA.at[1]], out)
 
     for copy in [*mz, *mf, *ms.values(), *zs.values(), *zr.values(), *far.values(), *adj.values(), *ff.values(), *fa.values()]:
         copy.wait_send()
@@ -376,14 +425,13 @@
     return pl.pallas_call(
         kernel,
         name="routed_experts",
-        out_shape=jax.ShapeDtypeStruct((TOK, D), BF),
+        out_shape=pltpu.VMEM((TOK, D), BF),
         in_specs=[anywhere] * 6,
         out_specs=pl.BlockSpec(memory_space=pltpu.VMEM),
         scratch_shapes=[
             pltpu.VMEM((2, D, FF), BF),
             pltpu.VMEM((2, D, FF), BF),
             pltpu.VMEM((2, FF, D), BF),
-            pltpu.VMEM((2, TOK, 8), jnp.int32),
             pltpu.VMEM((4, 4, 2, HALF, D), BF),
             pltpu.VMEM((2, 4, 4, 16, TOK), jnp.int32),
             pltpu.VMEM((4, 2, 4, 2, CAP, D), BF),
@@ -403,9 +451,9 @@
             pltpu.SemaphoreType.DMA((3, 2)),
         ],
         compiler_params=pltpu.CompilerParams(
-            collective_id=0, has_side_effects=True, vmem_limit_bytes=67043328
+            collective_id=0, has_side_effects=True, vmem_limit_bytes=62 * 1024 * 1024
         ),
-    )(tokens.reshape(2, HALF, D), expert_ids, gate_nums, w_gate, w_up, w_down)
+    )(tokens.reshape(2, HALF, D), expert_ids.T, gate_nums.T, w_gate, w_up, w_down)
 
 
 def solution(mesh):

time: 123 us -> 115 us (0.935)
  Pallas kernels: 118 us -> 113 us
  local copies, waits for them, and re-layouts: 4.7 us -> 0.8 us
    pallas_call x1, Pallas kernels: 118 us -> 113 us  [shards(): pl.pallas_call(kernel, name='routed_experts', out_shape=pltpu.VMEM((TOK,...]
    unnamed x3 -> x1, local copies, waits for them, and re-layouts: 4.7 us -> 0.8 us
where the time goes in v2:
time: 115 us; the launch traced here: 114 us
  Pallas kernels  113 us (98%)
    pallas_call x1, Pallas kernels, shards(): pl.pallas_call(kernel, name='routed_experts', out_shape=pltpu.VMEM((TOK,...  113 us

profile of v2, /device:TPU:0, one launch (start us, length us, event | category | flops | bytes accessed | tf_op | source)
XLA Modules:
  0.0 114.0 jit_solution(17707706426442274204)
XLA Ops:
  0.0 113.2 %routed_experts.1 = bf16[128,2048]{1,0:T(8,128)(2,1)S(1)} custom-call(bf16[2,64,2048]{2,1,0:T(8,128)(2,1)} %bitcast.3, s32[8,128]{1,0:T(8,128)} %bitcast.4, s32[8,128]{1,0:T(8,128)} %bitcast.5, bf16[2,2048,768]{2,1,0:T(8,128)(2,1)} %wg_in.1, bf16[2,2048,768]{2,1,0:T(8,128)(2,1)} %wu_in.1, bf16[2,768,2048]{2,1,0:T(8,128)(2,1)} %wd_in.1), custom_call_target="tpu_custom_call" | custom-call | tf_op jit(solution)/shard_map/routed_experts/pallas_call | solution.py:425
  113.2 0.8 copy.8

commit v3 on v2

--- a/solution.py
+++ b/solution.py
@@ -86,14 +86,15 @@
         2: remote(M.at[0, 0], M.at[0, 2], "b2"),
     }
     mz = [remote(M.at[0, j], M.at[1, j], "z") for j in range(4)]
-    f = {
-        (3, 0): remote(T.at[0, 0, 0], T.at[0, 3, 0], "a+"),
-        (1, 1): remote(T.at[0, 0, 1], T.at[0, 1, 1], "a+"),
-        (2, 0): remote(T.at[0, 3, 0], T.at[0, 2, 0], "a+"),
-        (3, 1): remote(T.at[0, 0, 1], T.at[0, 3, 1], "a-"),
-        (1, 0): remote(T.at[0, 0, 0], T.at[0, 1, 0], "a-"),
-        (2, 1): remote(T.at[0, 3, 1], T.at[0, 2, 1], "a-"),
-    }
+    f = {}
+    for q in range(2):
+        part = pl.ds(32 * q, 32)
+        f[3, 0, q] = remote(T.at[0, 0, 0, part], T.at[0, 3, 0, part], "a+")
+        f[1, 1, q] = remote(T.at[0, 0, 1, part], T.at[0, 1, 1, part], "a+")
+        f[2, 0, q] = remote(T.at[0, 3, 0, part], T.at[0, 2, 0, part], "a+")
+        f[3, 1, q] = remote(T.at[0, 0, 1, part], T.at[0, 3, 1, part], "a-")
+        f[1, 0, q] = remote(T.at[0, 0, 0, part], T.at[0, 1, 0, part], "a-")
+        f[2, 1, q] = remote(T.at[0, 3, 1, part], T.at[0, 2, 1, part], "a-")
     s = {}
     for i in range(4):
         s[2, i, 0] = remote(T.at[0, i, 0], T.at[2, i, 0], "b+")
@@ -102,8 +103,17 @@
         s[1, i, 1] = remote(T.at[2, i, 1], T.at[1, i, 1], "b-")
         s[3, i, 1] = remote(T.at[0, i, 1], T.at[3, i, 1], "b+")
         s[3, i, 0] = remote(T.at[0, i, 0], T.at[3, i, 0], "b-")
-    zs = {(c, i): remote(ZS.at[c, i], X.at[c, 1, i], "z") for c in range(4) for i in range(4)}
-    zr = {(c, i): remote(X.at[c, 1, i], YR.at[c, i], "z") for c in range(4) for i in range(4)}
+    zs = {(c, i): remote(ZS.at[c, i], X.at[c, 1, i], "z") for c in range(4) for i in range(4) if c or not i}
+    zq = {}
+    for i in range(1, 4):
+        for q in range(2):
+            part = pl.ds(16 * q, 16)
+            zq[i, q] = remote(ZS.at[0, i, :, part], X.at[0, 1, i, :, part], "z")
+    zr = {(c, i): remote(X.at[c, 1, i], YR.at[c, i], "z") for c in range(4) for i in range(4) if (c, i) != (0, 1)}
+    zl = []
+    for q in range(2):
+        part = pl.ds(16 * q, 16)
+        zl.append(remote(X.at[0, 1, 1, :, part], YR.at[0, 1, :, part], "z"))
     far = {}
     adj = {}
     for i in range(4):
@@ -118,11 +128,13 @@
         1: remote(T.at[0, 2, 1], FFR.at[1], "a-"),
     }
     fa = {
-        (1, 0): remote(T.at[0, 1, 0], FA.at[0, 0], "a+"),
         (3, 1): remote(T.at[0, 3, 1], FA.at[0, 1], "a+"),
         (3, 0): remote(T.at[0, 3, 0], FA.at[1, 0], "a-"),
-        (1, 1): remote(T.at[0, 1, 1], FA.at[1, 1], "a-"),
     }
+    for q in range(2):
+        part = pl.ds(32 * q, 32)
+        fa[1, 0, q] = remote(T.at[0, 1, 0, part], FA.at[0, 0, part], "a+")
+        fa[1, 1, q] = remote(T.at[0, 1, 1, part], FA.at[1, 1, part], "a-")
 
     barrier = pltpu.get_barrier_semaphore()
     peers = ("a+", "a-", "a2", "b+", "b-", "b2", "z")
@@ -142,7 +154,7 @@
     lane8 = lax.broadcasted_iota(jnp.int32, (8, TOK), 1)
     sub32 = lax.broadcasted_iota(jnp.int32, (CAP, TOK), 0).astype(F32)
     expert = jnp.where(sub8 < 2, 2 * ep + sub8, 2 * pep + sub8 - 2)
-    start_slot = ((lane8 & 96) >> 2).astype(F32)
+    start_slot = (((lane8 & 32) >> 1) + ((lane8 & 64) >> 3)).astype(F32)
 
     low = lax.broadcasted_iota(jnp.int32, (16, TOK), 1) < HALF
 
@@ -166,18 +178,34 @@
             column = jnp.sum(jnp.where(hits[e], gate[e : e + 1], 0.0), axis=1, keepdims=True)
             G[c, e, plane, i] = jnp.broadcast_to(column, (CAP, TOK))
 
-    def pack(c, i):
+    def place(c, i):
         code, gate = slots_of(pick(c, i, 0))
         hits = [sub32 == code[r : r + 1] for r in range(4)]
         places = jnp.concatenate([jnp.where(hits[r], 1.0, 0.0) for r in range(4)], axis=0).astype(BF)
         PS[c, i] = places
+        weigh(c, i, 0, hits, gate)
+        return places
+
+    def pack(c, i):
+        places = place(c, i)
         for n in range(4):
             cols = slice(512 * n, 512 * n + 512)
             rows = T[c, i, :, :, cols].reshape(TOK, 512)
             packed = jnp.dot(places, rows, preferred_element_type=F32).astype(BF)
             X[c, 0, i, :, :, cols] = packed[:HALF].reshape(2, CAP, 512)
             ZS[c, i, :, :, cols] = packed[HALF:].reshape(2, CAP, 512)
-        weigh(c, i, 0, hits, gate)
+
+    def pack_quarter(i, q):
+        part, own = slice(16 * q, 16 * q + 16), slice(32 * q, 32 * q + 32)
+        places = jnp.concatenate([PS[0, i, 32 * r + 16 * q : 32 * r + 16 * q + 16] for r in range(4)], axis=0)
+        for n in range(4):
+            cols = slice(512 * n, 512 * n + 512)
+            first, second = T[0, i, 0, own, cols], T[0, i, 1, own, cols]
+            rows = jnp.concatenate([first, first, second, second], axis=0)
+            packed = jnp.dot(places, rows, preferred_element_type=F32).astype(BF)
+            X[0, 0, i, :, part, cols] = packed[:32].reshape(2, 16, 512)
+            ZS[0, i, :, part, cols] = packed[32:].reshape(2, 16, 512)
+        zq[i, q].start()
 
     def weigh_theirs(c):
         for i in range(4):
@@ -205,8 +233,8 @@
         lax.fori_loop(low, high, body, 0)
 
     def arrived(c):
-        for i in ORDER:
-            zs[c, i].wait_recv()
+        for copy in [zs[0, 0], *zq.values()] if c == 0 else [zs[c, i] for i in ORDER]:
+            copy.wait_recv()
         weigh_theirs(c)
 
     def fine(c, e):
@@ -289,37 +317,46 @@
 
     pack(0, 0)
     pl.semaphore_wait(barrier, len(peers))
-    f[3, 0].start()
-    f[3, 1].start()
-    for copy in mf:
-        copy.start()
-    zs[0, 0].start()
-    f[1, 1].start()
-    f[1, 0].start()
-    f[3, 0].wait_recv()
-    f[2, 0].start()
-    f[3, 1].wait_recv()
-    f[2, 1].start()
-    for copy in mf:
-        copy.wait_recv()
-    for j in (1, 3, 2):
-        ms[j].start()
-    pack_send(0, 3)
+    for q in range(2):
+        f[3, 0, q].start()
+        f[3, 1, q].start()
+        if q == 0:
+            for copy in mf:
+                copy.start()
+            zs[0, 0].start()
+    for q in range(2):
+        f[1, 1, q].start()
+        f[1, 0, q].start()
+    for q in range(2):
+        for h in range(2):
+            f[3, h, q].wait_recv()
+            f[2, h, q].start()
+        if q == 0:
+            for copy in mf:
+                copy.wait_recv()
+            place(0, 3)
+            for j in (1, 3, 2):
+                ms[j].start()
+        pack_quarter(3, q)
+    place(0, 1)
+    for q in range(2):
+        for h in range(2):
+            f[1, h, q].wait_recv()
+        for i in ((), (0, 3, 1))[q]:
+            s[2, i, 0].start()
+            s[2, i, 1].start()
+        pack_quarter(1, q)
     mz[0].start()
-    f[1, 0].wait_recv()
-    f[1, 1].wait_recv()
-    for i in (0, 3, 1):
-        s[2, i, 0].start()
-        s[2, i, 1].start()
-    pack_send(0, 1)
-    f[2, 0].wait_recv()
-    f[2, 1].wait_recv()
-    pack_send(0, 2)
-    s[2, 2, 0].start()
-    s[2, 2, 1].start()
     for j in (1, 3, 2):
         ms[j].wait_recv()
         mz[j].start()
+    place(0, 2)
+    for q in range(2):
+        for h in range(2):
+            f[2, h, q].wait_recv()
+        pack_quarter(2, q)
+    s[2, 2, 0].start()
+    s[2, 2, 1].start()
     near(0)
     near(3)
     others(0)
@@ -397,27 +434,45 @@
     finish(2, [])
     ff[0].start()
     ff[1].start()
-    zr[0, 1].start()
+    zl[0].start()
+    zl[1].start()
     returned(3, 1)
     zr[0, 0].start()
     finish(3, [])
     fa[3, 0].start()
     fa[3, 1].start()
     returned(3, 0)
+    for c in (2, 3):
+        for h in range(2):
+            adj[c, 1, h].wait_recv()
     ff[0].wait_recv()
     ff[1].wait_recv()
-    finish(1, [FFR])
-    fa[1, 0].start()
-    fa[1, 1].start()
+    for q in range(2):
+        zl[q].wait_recv()
+        part, own = slice(16 * q, 16 * q + 16), slice(32 * q, 32 * q + 32)
+        places = jnp.concatenate([PS[0, 1, 32 * r + 16 * q : 32 * r + 16 * q + 16] for r in range(4)], axis=0)
+        for n in range(4):
+            cols = slice(512 * n, 512 * n + 512)
+            y = jnp.concatenate(
+                [X[0, 0, 1, :, part, cols].reshape(32, 512), YR[0, 1, :, part, cols].reshape(32, 512)], axis=0
+            )
+            total = lax.dot_general(places, y, (((0,), (0,)), ((), ())), preferred_element_type=F32)
+            for h in range(2):
+                rows = total[64 * h + 32 * q : 64 * h + 32 * q + 32]
+                for ref in (ADJ.at[0, 1, h], ADJ.at[1, 1, h], FFR.at[h]):
+                    rows = rows + ref[own, cols].astype(F32)
+                T[0, 1, h, own, cols] = rows.astype(BF)
+        fa[1, 0, q].start()
+        fa[1, 1, q].start()
     for copy in fa.values():
         copy.wait_recv()
     finish(0, [FA.at[0], FA.at[1]], out)
 
-    for copy in [*mz, *mf, *ms.values(), *zs.values(), *zr.values(), *far.values(), *adj.values(), *ff.values(), *fa.values()]:
+    for copy in [*mz, *mf, *ms.values(), *zs.values(), *zq.values(), *zl, *zr.values(), *far.values(), *adj.values(), *ff.values(), *fa.values()]:
         copy.wait_send()
 
 
-COPIES = 10 + 6 + 24 + 16 + 16 + 8 + 16 + 2 + 4
+COPIES = 10 + 12 + 24 + 13 + 6 + 17 + 8 + 16 + 2 + 6
 
 
 def shards(tokens, expert_ids, gate_nums, w_gate, w_up, w_down):

time: 115 us -> 112 us (0.974)
  Pallas kernels: 113 us -> 111 us
    pallas_call x1, Pallas kernels: 113 us -> 111 us  [shards(): pl.pallas_call(kernel, name='routed_experts', out_shape=pltpu.VMEM((TOK,...]
where the time goes in v3:
time: 112 us; the launch traced here: 111 us
  Pallas kernels  111 us (99%)
    pallas_call x1, Pallas kernels, shards(): pl.pallas_call(kernel, name='routed_experts', out_shape=pltpu.VMEM((TOK,...  111 us

profile of v3, /device:TPU:0, one launch (start us, length us, event | category | flops | bytes accessed | tf_op | source)
XLA Modules:
  0.0 111.3 jit_solution(6331763307927739151)
XLA Ops:
  0.0 110.5 %routed_experts.1 = bf16[128,2048]{1,0:T(8,128)(2,1)S(1)} custom-call(bf16[2,64,2048]{2,1,0:T(8,128)(2,1)} %bitcast.3, s32[8,128]{1,0:T(8,128)} %bitcast.4, s32[8,128]{1,0:T(8,128)} %bitcast.5, bf16[2,2048,768]{2,1,0:T(8,128)(2,1)} %wg_in.1, bf16[2,2048,768]{2,1,0:T(8,128)(2,1)} %wu_in.1, bf16[2,768,2048]{2,1,0:T(8,128)(2,1)} %wd_in.1), custom_call_target="tpu_custom_call" | custom-call | tf_op jit(solution)/shard_map/routed_experts/pallas_call | solution.py:480
  110.6 0.8 copy.8

commit v4 on v3

--- a/solution.py
+++ b/solution.py
@@ -51,19 +51,26 @@
     send, recv, local, wsem,
 ):
     where, ep, pep = neighbours()
-    counter = [0]
-
-    def remote(src, dst, to):
-        index = counter[0]
-        counter[0] += 1
+    leaving, landing = {}, {}
+
+    def remote(src, dst, to, group, key):
         return pltpu.make_async_remote_copy(
-            src_ref=src, dst_ref=dst, send_sem=send.at[index], recv_sem=recv.at[index],
-            device_id=where[to], device_id_type=MESH,
+            src_ref=src,
+            dst_ref=dst,
+            send_sem=send.at[leaving.setdefault(group, len(leaving))],
+            recv_sem=recv.at[landing.setdefault(key, len(landing))],
+            device_id=where[to],
+            device_id_type=MESH,
         )
 
+    def sent(group, ref):
+        pltpu.make_async_copy(ref, ref, send.at[leaving[group]]).wait()
+
+    def landed(key, ref):
+        pltpu.make_async_copy(ref, ref, recv.at[landing[key]]).wait()
+
     loads = [
-        pltpu.make_async_copy(src.at[e], dst.at[e], wsem.at[k, e])
-        for e in range(2)
+        pltpu.make_async_copy(src, dst, wsem.at[k])
         for k, (src, dst) in enumerate(((wg_in, wg), (wu_in, wu), (wd_in, wd)))
     ]
     own = pltpu.make_async_copy(tokens, T.at[0, 0], local.at[0])
@@ -76,65 +83,65 @@
         table.start()
 
     mf = [
-        remote(M.at[0, 0, 0], M.at[0, 0, 3], "a+"),
-        remote(M.at[0, 0, 0], M.at[0, 0, 1], "a-"),
-        remote(M.at[0, 0, 0], M.at[0, 0, 2], "a2"),
+        remote(M.at[0, 0, 0], M.at[0, 0, 3], "a+", "mf", "mf"),
+        remote(M.at[0, 0, 0], M.at[0, 0, 1], "a-", "mf", "mf"),
+        remote(M.at[0, 0, 0], M.at[0, 0, 2], "a2", "mf", "mf"),
     ]
     ms = {
-        3: remote(M.at[0, 0], M.at[0, 3], "b+"),
-        1: remote(M.at[0, 0], M.at[0, 1], "b-"),
-        2: remote(M.at[0, 0], M.at[0, 2], "b2"),
+        3: remote(M.at[0, 0], M.at[0, 3], "b+", "ms", "ms"),
+        1: remote(M.at[0, 0], M.at[0, 1], "b-", "ms", "ms"),
+        2: remote(M.at[0, 0], M.at[0, 2], "b2", "ms", "ms"),
     }
-    mz = [remote(M.at[0, j], M.at[1, j], "z") for j in range(4)]
+    mz = [remote(M.at[0, j], M.at[1, j], "z", "mz", "mz") for j in range(4)]
     f = {}
     for q in range(2):
         part = pl.ds(32 * q, 32)
-        f[3, 0, q] = remote(T.at[0, 0, 0, part], T.at[0, 3, 0, part], "a+")
-        f[1, 1, q] = remote(T.at[0, 0, 1, part], T.at[0, 1, 1, part], "a+")
-        f[2, 0, q] = remote(T.at[0, 3, 0, part], T.at[0, 2, 0, part], "a+")
-        f[3, 1, q] = remote(T.at[0, 0, 1, part], T.at[0, 3, 1, part], "a-")
-        f[1, 0, q] = remote(T.at[0, 0, 0, part], T.at[0, 1, 0, part], "a-")
-        f[2, 1, q] = remote(T.at[0, 3, 1, part], T.at[0, 2, 1, part], "a-")
+        f[3, 0, q] = remote(T.at[0, 0, 0, part], T.at[0, 3, 0, part], "a+", "f", ("f", 3, q))
+        f[1, 1, q] = remote(T.at[0, 0, 1, part], T.at[0, 1, 1, part], "a+", "f", ("f", 1, q))
+        f[2, 0, q] = remote(T.at[0, 3, 0, part], T.at[0, 2, 0, part], "a+", "f", ("f", 2, q))
+        f[3, 1, q] = remote(T.at[0, 0, 1, part], T.at[0, 3, 1, part], "a-", "f", ("f", 3, q))
+        f[1, 0, q] = remote(T.at[0, 0, 0, part], T.at[0, 1, 0, part], "a-", "f", ("f", 1, q))
+        f[2, 1, q] = remote(T.at[0, 3, 1, part], T.at[0, 2, 1, part], "a-", "f", ("f", 2, q))
     s = {}
     for i in range(4):
-        s[2, i, 0] = remote(T.at[0, i, 0], T.at[2, i, 0], "b+")
-        s[2, i, 1] = remote(T.at[0, i, 1], T.at[2, i, 1], "b-")
-        s[1, i, 0] = remote(T.at[2, i, 0], T.at[1, i, 0], "b+")
-        s[1, i, 1] = remote(T.at[2, i, 1], T.at[1, i, 1], "b-")
-        s[3, i, 1] = remote(T.at[0, i, 1], T.at[3, i, 1], "b+")
-        s[3, i, 0] = remote(T.at[0, i, 0], T.at[3, i, 0], "b-")
-    zs = {(c, i): remote(ZS.at[c, i], X.at[c, 1, i], "z") for c in range(4) for i in range(4) if c or not i}
+        s[2, i, 0] = remote(T.at[0, i, 0], T.at[2, i, 0], "b+", "s", ("s", 2, i))
+        s[2, i, 1] = remote(T.at[0, i, 1], T.at[2, i, 1], "b-", "s", ("s", 2, i))
+        s[1, i, 0] = remote(T.at[2, i, 0], T.at[1, i, 0], "b+", "s", ("s", 1, i))
+        s[1, i, 1] = remote(T.at[2, i, 1], T.at[1, i, 1], "b-", "s", ("s", 1, i))
+        s[3, i, 1] = remote(T.at[0, i, 1], T.at[3, i, 1], "b+", "s", ("s", 3, i))
+        s[3, i, 0] = remote(T.at[0, i, 0], T.at[3, i, 0], "b-", "s", ("s", 3, i))
+    zs = {(c, i): remote(ZS.at[c, i], X.at[c, 1, i], "z", "zs", ("zs", c)) for c in range(4) for i in range(4) if c or not i}
     zq = {}
     for i in range(1, 4):
         for q in range(2):
             part = pl.ds(16 * q, 16)
-            zq[i, q] = remote(ZS.at[0, i, :, part], X.at[0, 1, i, :, part], "z")
-    zr = {(c, i): remote(X.at[c, 1, i], YR.at[c, i], "z") for c in range(4) for i in range(4) if (c, i) != (0, 1)}
+            zq[i, q] = remote(ZS.at[0, i, :, part], X.at[0, 1, i, :, part], "z", "zs", ("zs", 0))
+    zr = {(c, i): remote(X.at[c, 1, i], YR.at[c, i], "z", "zr", ("zr", c, i)) for c in range(4) for i in range(4) if (c, i) != (0, 1)}
     zl = []
     for q in range(2):
         part = pl.ds(16 * q, 16)
-        zl.append(remote(X.at[0, 1, 1, :, part], YR.at[0, 1, :, part], "z"))
+        zl.append(remote(X.at[0, 1, 1, :, part], YR.at[0, 1, :, part], "z", "zr", ("zl", q)))
     far = {}
     adj = {}
     for i in range(4):
-        far[i, 0] = remote(T.at[1, i, 0], FAR.at[i, 0], "b+")
-        far[i, 1] = remote(T.at[1, i, 1], FAR.at[i, 1], "b-")
-        adj[2, i, 0] = remote(T.at[2, i, 0], ADJ.at[1, i, 0], "b-")
-        adj[2, i, 1] = remote(T.at[2, i, 1], ADJ.at[0, i, 1], "b+")
-        adj[3, i, 0] = remote(T.at[3, i, 0], ADJ.at[0, i, 0], "b+")
-        adj[3, i, 1] = remote(T.at[3, i, 1], ADJ.at[1, i, 1], "b-")
+        far[i, 0] = remote(T.at[1, i, 0], FAR.at[i, 0], "b+", "far", ("far", i))
+        far[i, 1] = remote(T.at[1, i, 1], FAR.at[i, 1], "b-", "far", ("far", i))
+        adj[2, i, 0] = remote(T.at[2, i, 0], ADJ.at[1, i, 0], "b-", "adj", ("adj", i))
+        adj[2, i, 1] = remote(T.at[2, i, 1], ADJ.at[0, i, 1], "b+", "adj", ("adj", i))
+        adj[3, i, 0] = remote(T.at[3, i, 0], ADJ.at[0, i, 0], "b+", "adj", ("adj", i))
+        adj[3, i, 1] = remote(T.at[3, i, 1], ADJ.at[1, i, 1], "b-", "adj", ("adj", i))
     ff = {
-        0: remote(T.at[0, 2, 0], FFR.at[0], "a+"),
-        1: remote(T.at[0, 2, 1], FFR.at[1], "a-"),
+        0: remote(T.at[0, 2, 0], FFR.at[0], "a+", "ff", "ff"),
+        1: remote(T.at[0, 2, 1], FFR.at[1], "a-", "ff", "ff"),
     }
     fa = {
-        (3, 1): remote(T.at[0, 3, 1], FA.at[0, 1], "a+"),
-        (3, 0): remote(T.at[0, 3, 0], FA.at[1, 0], "a-"),
+        (3, 1): remote(T.at[0, 3, 1], FA.at[0, 1], "a+", "fa", "fa"),
+        (3, 0): remote(T.at[0, 3, 0], FA.at[1, 0], "a-", "fa", "fa"),
     }
     for q in range(2):
         part = pl.ds(32 * q, 32)
-        fa[1, 0, q] = remote(T.at[0, 1, 0, part], FA.at[0, 0, part], "a+")
-        fa[1, 1, q] = remote(T.at[0, 1, 1, part], FA.at[1, 1, part], "a-")
+        fa[1, 0, q] = remote(T.at[0, 1, 0, part], FA.at[0, 0, part], "a+", "fa", "fa")
+        fa[1, 1, q] = remote(T.at[0, 1, 1, part], FA.at[1, 1, part], "a-", "fa", "fa")
 
     barrier = pltpu.get_barrier_semaphore()
     peers = ("a+", "a-", "a2", "b+", "b-", "b2", "z")
@@ -187,7 +194,7 @@
         return places
 
     def pack(c, i):
-        places = place(c, i)
+        places = PS[c, i]
         for n in range(4):
             cols = slice(512 * n, 512 * n + 512)
             rows = T[c, i, :, :, cols].reshape(TOK, 512)
@@ -233,8 +240,7 @@
         lax.fori_loop(low, high, body, 0)
 
     def arrived(c):
-        for copy in [zs[0, 0], *zq.values()] if c == 0 else [zs[c, i] for i in ORDER]:
-            copy.wait_recv()
+        landed(("zs", c), X.at[c, 1])
         weigh_theirs(c)
 
     def fine(c, e):
@@ -266,31 +272,11 @@
             else:
                 target[:, cols] = total.astype(BF)
 
-    def pack_send(c, i):
-        pack(c, i)
-        zs[c, i].start()
-
-    def near(i):
-        for h in range(2):
-            s[2, i, h].wait_recv()
-            s[1, i, h].start()
-        pack_send(2, i)
-
-    def others(i):
-        s[3, i, 1].start()
-        s[3, i, 0].start()
-
-    def distant(c, i):
-        s[c, i, 0].wait_recv()
-        s[c, i, 1].wait_recv()
-        pack_send(c, i)
-
     def returned(c, i):
-        zr[c, i].wait_recv()
+        landed(("zr", c, i), YR.at[c, i])
         extra = []
         if c == 3:
-            far[i, 0].wait_recv()
-            far[i, 1].wait_recv()
+            landed(("far", i), FAR.at[i])
             extra = [FAR.at[i]]
         combine(c, i, extra)
         for h in range(2):
@@ -301,20 +287,23 @@
         zs[c, i].start()
 
     def near(i):
+        landed(("s", 2, i), T.at[2, i])
         for h in range(2):
-            s[2, i, h].wait_recv()
             s[1, i, h].start()
         pack_send(2, i)
+        place(1, i)
 
     def others(i):
         s[3, i, 1].start()
         s[3, i, 0].start()
 
     def distant(c, i):
-        s[c, i, 0].wait_recv()
-        s[c, i, 1].wait_recv()
+        landed(("s", c, i), T.at[c, i])
         pack_send(c, i)
-
+        if c == 1:
+            place(3, i)
+
+    place(0, 0)
     pack(0, 0)
     pl.semaphore_wait(barrier, len(peers))
     for q in range(2):
@@ -328,32 +317,31 @@
         f[1, 1, q].start()
         f[1, 0, q].start()
     for q in range(2):
+        landed(("f", 3, q), T.at[0, 3, :, pl.ds(32 * q, 32)])
         for h in range(2):
-            f[3, h, q].wait_recv()
             f[2, h, q].start()
         if q == 0:
-            for copy in mf:
-                copy.wait_recv()
+            landed("mf", M.at[0, 0, pl.ds(1, 3)])
             place(0, 3)
             for j in (1, 3, 2):
                 ms[j].start()
         pack_quarter(3, q)
     place(0, 1)
     for q in range(2):
-        for h in range(2):
-            f[1, h, q].wait_recv()
+        landed(("f", 1, q), T.at[0, 1, :, pl.ds(32 * q, 32)])
         for i in ((), (0, 3, 1))[q]:
             s[2, i, 0].start()
             s[2, i, 1].start()
         pack_quarter(1, q)
     mz[0].start()
+    landed("ms", M.at[0, pl.ds(1, 3)])
     for j in (1, 3, 2):
-        ms[j].wait_recv()
         mz[j].start()
     place(0, 2)
-    for q in range(2):
-        for h in range(2):
-            f[2, h, q].wait_recv()
+    for i in ORDER:
+        place(2, i)
+    for q in range(2):
+        landed(("f", 2, q), T.at[0, 2, :, pl.ds(32 * q, 32)])
         pack_quarter(2, q)
     s[2, 2, 0].start()
     s[2, 2, 1].start()
@@ -366,8 +354,7 @@
     others(1)
     others(2)
     distant(1, 0)
-    for copy in mz:
-        copy.wait_recv()
+    landed("mz", M.at[1])
     for load in loads:
         load.wait()
     arrived(0)
@@ -391,14 +378,13 @@
     run(second)
     for i in BACK:
         zr[2, i].start()
-    for copy in list(f.values()) + list(s.values()):
-        copy.wait_send()
+    sent("f", T.at[0, pl.ds(0, 3)])
+    sent("s", T.at[pl.ds(0, 3)])
     arrived(1)
     run(coarse(1, 0) + coarse(1, 1))
-    for i, k in zip(ORDER, BACK):
-        zs[3, i].wait_recv()
-        zr[1, k].start()
-    weigh_theirs(3)
+    arrived(3)
+    for i in BACK:
+        zr[1, i].start()
     returned(2, 2)
     third = coarse(3, 0) + coarse(3, 1)
     run(third, 1)
@@ -421,10 +407,8 @@
     zr[3, 1].start()
 
     def finish(i, extra, target=None):
-        zr[0, i].wait_recv()
-        for c in (2, 3):
-            adj[c, i, 0].wait_recv()
-            adj[c, i, 1].wait_recv()
+        landed(("zr", 0, i), YR.at[0, i])
+        landed(("adj", i), ADJ.at[:, i])
         combine(0, i, [ADJ.at[0, i], ADJ.at[1, i]] + extra, target)
 
     returned(3, 2)
@@ -442,13 +426,10 @@
     fa[3, 0].start()
     fa[3, 1].start()
     returned(3, 0)
-    for c in (2, 3):
-        for h in range(2):
-            adj[c, 1, h].wait_recv()
-    ff[0].wait_recv()
-    ff[1].wait_recv()
-    for q in range(2):
-        zl[q].wait_recv()
+    landed(("adj", 1), ADJ.at[:, 1])
+    landed("ff", FFR)
+    for q in range(2):
+        landed(("zl", q), YR.at[0, 1, :, pl.ds(16 * q, 16)])
         part, own = slice(16 * q, 16 * q + 16), slice(32 * q, 32 * q + 32)
         places = jnp.concatenate([PS[0, 1, 32 * r + 16 * q : 32 * r + 16 * q + 16] for r in range(4)], axis=0)
         for n in range(4):
@@ -464,15 +445,18 @@
                 T[0, 1, h, own, cols] = rows.astype(BF)
         fa[1, 0, q].start()
         fa[1, 1, q].start()
-    for copy in fa.values():
-        copy.wait_recv()
+    landed("fa", FA)
     finish(0, [FA.at[0], FA.at[1]], out)
 
-    for copy in [*mz, *mf, *ms.values(), *zs.values(), *zq.values(), *zl, *zr.values(), *far.values(), *adj.values(), *ff.values(), *fa.values()]:
-        copy.wait_send()
-
-
-COPIES = 10 + 12 + 24 + 13 + 6 + 17 + 8 + 16 + 2 + 6
+    for group, ref in (
+        ("mf", M.at[0, 0, pl.ds(0, 3)]), ("ms", M.at[0, pl.ds(0, 3)]), ("mz", M.at[0]), ("zs", ZS), ("zr", YR),
+        ("far", FAR), ("adj", ADJ), ("ff", FFR), ("fa", FA),
+    ):
+        sent(group, ref)
+
+
+GROUPS = 11
+KEYS = 3 + 6 + 12 + 4 + 17 + 4 + 4 + 2
 
 
 def shards(tokens, expert_ids, gate_nums, w_gate, w_up, w_down):
@@ -500,10 +484,10 @@
             pltpu.VMEM((2, HALF, D), BF),
             pltpu.VMEM((2, 2, HALF, D), BF),
             pltpu.VMEM((TOK, TOK), BF),
-            pltpu.SemaphoreType.DMA((COPIES,)),
-            pltpu.SemaphoreType.DMA((COPIES,)),
+            pltpu.SemaphoreType.DMA((GROUPS,)),
+            pltpu.SemaphoreType.DMA((KEYS,)),
             pltpu.SemaphoreType.DMA((3,)),
-            pltpu.SemaphoreType.DMA((3, 2)),
+            pltpu.SemaphoreType.DMA((3,)),
         ],
         compiler_params=pltpu.CompilerParams(
             collective_id=0, has_side_effects=True, vmem_limit_bytes=62 * 1024 * 1024

time: 112 us -> 110 us (0.982)
  Pallas kernels: 111 us -> 109 us
    pallas_call x1, Pallas kernels: 111 us -> 109 us  [shards(): pl.pallas_call(kernel, name='routed_experts', out_shape=pltpu.VMEM((TOK,...]
where the time goes in v4:
time: 110 us
  Pallas kernels  109 us (99%)
    pallas_call x1, Pallas kernels, shards(): pl.pallas_call(kernel, name='routed_experts', out_shape=pltpu.VMEM((TOK,...  109 us

profile of v4, /device:TPU:0, one launch (start us, length us, event | category | flops | bytes accessed | tf_op | source)
XLA Modules:
  0.0 109.7 jit_solution(6484999900803342691)
XLA Ops:
  0.0 108.9 %routed_experts.1 = bf16[128,2048]{1,0:T(8,128)(2,1)S(1)} custom-call(bf16[2,64,2048]{2,1,0:T(8,128)(2,1)} %bitcast.3, s32[8,128]{1,0:T(8,128)} %bitcast.4, s32[8,128]{1,0:T(8,128)} %bitcast.5, bf16[2,2048,768]{2,1,0:T(8,128)(2,1)} %wg_in.1, bf16[2,2048,768]{2,1,0:T(8,128)(2,1)} %wu_in.1, bf16[2,768,2048]{2,1,0:T(8,128)(2,1)} %wd_in.1), custom_call_target="tpu_custom_call" | custom-call | tf_op jit(solution)/shard_map/routed_experts/pallas_call | solution.py:464
  108.9 0.8 copy.8

commit v5 on v4

--- a/solution.py
+++ b/solution.py
@@ -403,8 +403,8 @@
     run(last)
     returned(1, 1)
     returned(1, 0)
+    zr[3, 1].start()
     zr[0, 2].start()
-    zr[3, 1].start()
 
     def finish(i, extra, target=None):
         landed(("zr", 0, i), YR.at[0, i])
@@ -412,20 +412,20 @@
         combine(0, i, [ADJ.at[0, i], ADJ.at[1, i]] + extra, target)
 
     returned(3, 2)
+    zr[3, 0].start()
+    returned(3, 3)
     zr[0, 3].start()
-    returned(3, 3)
-    zr[3, 0].start()
+    returned(3, 1)
+    zl[0].start()
+    zl[1].start()
     finish(2, [])
     ff[0].start()
     ff[1].start()
-    zl[0].start()
-    zl[1].start()
-    returned(3, 1)
     zr[0, 0].start()
+    returned(3, 0)
     finish(3, [])
     fa[3, 0].start()
     fa[3, 1].start()
-    returned(3, 0)
     landed(("adj", 1), ADJ.at[:, 1])
     landed("ff", FFR)
     for q in range(2):

time: 110 us -> 109 us (level)
  Pallas kernels: 109 us -> 107 us
    pallas_call x1, Pallas kernels: 109 us -> 107 us  [shards(): pl.pallas_call(kernel, name='routed_experts', out_shape=pltpu.VMEM((TOK,...]
where the time goes in v5:
time: 109 us; the launch traced here: 108 us
  Pallas kernels  107 us (98%)
    pallas_call x1, Pallas kernels, shards(): pl.pallas_call(kernel, name='routed_experts', out_shape=pltpu.VMEM((TOK,...  107 us

profile of v5, /device:TPU:0, one launch (start us, length us, event | category | flops | bytes accessed | tf_op | source)
XLA Modules:
  0.0 108.1 jit_solution(7970074154733715895)
XLA Ops:
  0.0 107.3 %routed_experts.1 = bf16[128,2048]{1,0:T(8,128)(2,1)S(1)} custom-call(bf16[2,64,2048]{2,1,0:T(8,128)(2,1)} %bitcast.3, s32[8,128]{1,0:T(8,128)} %bitcast.4, s32[8,128]{1,0:T(8,128)} %bitcast.5, bf16[2,2048,768]{2,1,0:T(8,128)(2,1)} %wg_in.1, bf16[2,2048,768]{2,1,0:T(8,128)(2,1)} %wu_in.1, bf16[2,768,2048]{2,1,0:T(8,128)(2,1)} %wd_in.1), custom_call_target="tpu_custom_call" | custom-call | tf_op jit(solution)/shard_map/routed_experts/pallas_call | solution.py:464
  107.3 0.8 copy.8

commit v6 on v5

--- a/solution.py
+++ b/solution.py
@@ -47,7 +47,7 @@
 
 def kernel(
     tokens, ids_in, nums_in, wg_in, wu_in, wd_in, out,
-    wg, wu, wd, T, M, X, ZS, YR, PS, G, H, FAR, ADJ, FFR, FA, TRI,
+    wg, wu, wd, T, M, X, ZS, YR, PS, G, H, FAR, ADJ, FFR, FA, SUM, TRI,
     send, recv, local, wsem,
 ):
     where, ep, pep = neighbours()
@@ -270,7 +270,7 @@
             if target is None:
                 T[c, i, :, :, cols] = total.astype(BF).reshape(2, HALF, 512)
             else:
-                target[:, cols] = total.astype(BF)
+                target[:, :, cols] = total.reshape(2, HALF, 512)
 
     def returned(c, i):
         landed(("zr", c, i), YR.at[c, i])
@@ -428,6 +428,10 @@
     fa[3, 1].start()
     landed(("adj", 1), ADJ.at[:, 1])
     landed("ff", FFR)
+    for n in range(4):
+        cols = slice(512 * n, 512 * n + 512)
+        known = [ref[:, :, cols].astype(F32) for ref in (ADJ.at[0, 1], ADJ.at[1, 1], FFR)]
+        SUM[:, :, cols] = known[0] + known[1] + known[2]
     for q in range(2):
         landed(("zl", q), YR.at[0, 1, :, pl.ds(16 * q, 16)])
         part, own = slice(16 * q, 16 * q + 16), slice(32 * q, 32 * q + 32)
@@ -440,13 +444,15 @@
             total = lax.dot_general(places, y, (((0,), (0,)), ((), ())), preferred_element_type=F32)
             for h in range(2):
                 rows = total[64 * h + 32 * q : 64 * h + 32 * q + 32]
-                for ref in (ADJ.at[0, 1, h], ADJ.at[1, 1, h], FFR.at[h]):
-                    rows = rows + ref[own, cols].astype(F32)
-                T[0, 1, h, own, cols] = rows.astype(BF)
+                T[0, 1, h, own, cols] = (rows + SUM[h, own, cols]).astype(BF)
         fa[1, 0, q].start()
         fa[1, 1, q].start()
+    finish(0, [], SUM)
     landed("fa", FA)
-    finish(0, [FA.at[0], FA.at[1]], out)
+    for n in range(4):
+        cols = slice(512 * n, 512 * n + 512)
+        total = SUM[:, :, cols] + FA[0, :, :, cols].astype(F32) + FA[1, :, :, cols].astype(F32)
+        out[:, cols] = total.astype(BF).reshape(TOK, 512)
 
     for group, ref in (
         ("mf", M.at[0, 0, pl.ds(0, 3)]), ("ms", M.at[0, pl.ds(0, 3)]), ("mz", M.at[0]), ("zs", ZS), ("zr", YR),
@@ -483,6 +489,7 @@
             pltpu.VMEM((2, 4, 2, HALF, D), BF),
             pltpu.VMEM((2, HALF, D), BF),
             pltpu.VMEM((2, 2, HALF, D), BF),
+            pltpu.VMEM((2, HALF, D), F32),
             pltpu.VMEM((TOK, TOK), BF),
             pltpu.SemaphoreType.DMA((GROUPS,)),
             pltpu.SemaphoreType.DMA((KEYS,)),

time: 109 us -> 109 us (level)
  no operation moved by 1% of the time
where the time goes in v6:
time: 109 us; the launch traced here: 108 us
  Pallas kernels  107 us (98%)
    pallas_call x1, Pallas kernels, shards(): pl.pallas_call(kernel, name='routed_experts', out_shape=pltpu.VMEM((TOK,...  107 us

profile of v6, /device:TPU:0, one launch (start us, length us, event | category | flops | bytes accessed | tf_op | source)
XLA Modules:
  0.0 107.8 jit_solution(9925012875609107447)
XLA Ops:
  0.0 107.0 %routed_experts.1 = bf16[128,2048]{1,0:T(8,128)(2,1)S(1)} custom-call(bf16[2,64,2048]{2,1,0:T(8,128)(2,1)} %bitcast.3, s32[8,128]{1,0:T(8,128)} %bitcast.4, s32[8,128]{1,0:T(8,128)} %bitcast.5, bf16[2,2048,768]{2,1,0:T(8,128)(2,1)} %wg_in.1, bf16[2,2048,768]{2,1,0:T(8,128)(2,1)} %wu_in.1, bf16[2,768,2048]{2,1,0:T(8,128)(2,1)} %wd_in.1), custom_call_target="tpu_custom_call" | custom-call | tf_op jit(solution)/shard_map/routed_experts/pallas_call | solution.py:470
  107.0 0.8 copy.8

commit v7 on v6

--- a/solution.py
+++ b/solution.py
@@ -373,9 +373,8 @@
     distant(1, 2)
     run(second, 2)
     distant(3, 1)
-    run(second, 2)
+    run(second)
     distant(3, 2)
-    run(second)
     for i in BACK:
         zr[2, i].start()
     sent("f", T.at[0, pl.ds(0, 3)])

time: 109 us -> 109 us (level)
  no operation moved by 1% of the time
where the time goes in v7:
time: 109 us; the launch traced here: 108 us
  Pallas kernels  107 us (98%)
    pallas_call x1, Pallas kernels, shards(): pl.pallas_call(kernel, name='routed_experts', out_shape=pltpu.VMEM((TOK,...  107 us

profile of v7, /device:TPU:0, one launch (start us, length us, event | category | flops | bytes accessed | tf_op | source)
XLA Modules:
  0.0 107.8 jit_solution(6161686134881823765)
XLA Ops:
  0.0 107.0 %routed_experts.1 = bf16[128,2048]{1,0:T(8,128)(2,1)S(1)} custom-call(bf16[2,64,2048]{2,1,0:T(8,128)(2,1)} %bitcast.3, s32[8,128]{1,0:T(8,128)} %bitcast.4, s32[8,128]{1,0:T(8,128)} %bitcast.5, bf16[2,2048,768]{2,1,0:T(8,128)(2,1)} %wg_in.1, bf16[2,2048,768]{2,1,0:T(8,128)(2,1)} %wu_in.1, bf16[2,768,2048]{2,1,0:T(8,128)(2,1)} %wd_in.1), custom_call_target="tpu_custom_call" | custom-call | tf_op jit(solution)/shard_map/routed_experts/pallas_call | solution.py:469
  107.0 0.8 copy.8
